TPU v7x, 32 devices: a whole 2x2x4 slice. The times are simulated.
32 devices in a mesh: rows: 8 (over z, y), par: 4 (over x, core).
Axes of the slice: x: 2, y: 2, z: 4, core: 2. Of those that a mesh axis runs over, the one named last changes fastest.
Arguments:
- base_a: bfloat16 [4, 64, 256], P(None, 'rows'), may hold values from -6 to 6
- base_b: bfloat16 [4, 64, 256], P(None, 'rows'), may hold values from -6 to 6
- input_scale: float32 [256], replicated, may hold values from 0.1 to 3
- layer_one: bfloat16 [256, 1024], replicated, may hold values from -0.375 to 0.375
- layer_two: bfloat16 [1024, 1024], replicated, may hold values from -0.1875 to 0.1875
- layer_three: bfloat16 [1024, 128], replicated, may hold values from -0.1875 to 0.1875
- swap_cols: int32 [256], P('par'), may hold values from 0 to 255, each once
- window_ends: int32 [4], replicated, may hold values from 32 to 64
Outputs:
- first_order: float32 [4, 256, 128], P(None, 'par')
- total_order: float32 [4, 256, 128], P(None, 'par')
- total_variance: float32 [4, 128], replicated
Inputs may be any that keep to these rules, and one draw needn't show every extreme that they name: window w uses its rows 0 to window_ends[w] - 1. `swap_cols`: each column appears once.
All inputs are finite; a program needn't handle non-finite values.
Results may differ from a plain program's by a relative error of at most 0.0055.
The roundings to bfloat16 on the way count: a program that leaves them out, or rounds other values in their place, can miss the bound.
Values sent between devices are 32-bit elements; how exact they have to be, the bound alone decides.
A program may use at most 64 MiB of HBM per device.

v0:
```python
import jax
import jax.numpy as jnp
from jax import lax
from jax.sharding import PartitionSpec as P


def network_tail(first_pre, layer_two, layer_three):
    hidden_one = jax.nn.silu(first_pre).astype(jnp.bfloat16)
    second_pre = jnp.dot(hidden_one, layer_two, preferred_element_type=jnp.float32)
    hidden_two = jax.nn.silu(second_pre).astype(jnp.bfloat16)
    return jnp.dot(hidden_two, layer_three, preferred_element_type=jnp.float32)


def merge_total(former, latter):
    counts = former[0] + latter[0]
    inverse = 1.0 / jnp.maximum(counts, 1.0)
    change = latter[1] - former[1]
    return (
        counts,
        former[1] + change * latter[0] * inverse,
        former[2] + latter[2] + change * change * former[0] * latter[0] * inverse,
    )


def merge_groups(former, latter):
    counts = former[0] + latter[0]
    inverse = 1.0 / jnp.maximum(counts, 1.0)
    change_b = latter[1] - former[1]
    change_d = latter[2] - former[2]
    pair_weight = former[0] * latter[0] * inverse
    return (
        counts,
        former[1] + change_b * latter[0] * inverse,
        former[2] + change_d * latter[0] * inverse,
        former[3] + latter[3] + change_d * change_d * pair_weight,
        former[4] + latter[4] + change_b * change_d * pair_weight,
    )


def pick_window(states, window):
    return tuple((member[window : window + 1] for member in states))


def join_windows(*pieces):
    return jnp.concatenate(pieces, 0)


def conclude_states(total_state, group_state, windows):
    firsts = []
    totals = []
    variances = []
    running_total = None
    running_groups = None
    for window in range(windows):
        total_now = tuple((member[window] for member in total_state))
        group_now = tuple((member[window] for member in group_state))
        if window == 0:
            running_total = total_now
            running_groups = group_now
        else:
            running_total = merge_total(running_total, total_now)
            running_groups = merge_groups(running_groups, group_now)
        variance = running_total[2] / running_total[0]
        firsts.append(running_groups[4] / running_groups[0] / variance)
        totals.append(
            0.5
            * (running_groups[3] / running_groups[0] + running_groups[2] * running_groups[2])
            / variance
        )
        variances.append(variance)
    return (jnp.stack(firsts), jnp.stack(totals), jnp.stack(variances))


def local(base_a, base_b, input_scale, layer_one, layer_two, layer_three, swap_cols, window_ends):
    windows, window_rows, width = base_a.shape
    par_size = lax.axis_size("par")
    quarter = window_rows // par_size
    groups = swap_cols.shape[0]
    hidden = layer_one.shape[1]
    outputs = layer_three.shape[1]
    all_rows = windows * window_rows
    row_start = lax.axis_index("rows") * window_rows
    usable = (
        row_start + jnp.arange(window_rows, dtype=jnp.int32)[None, :] < window_ends[:, None]
    ).astype(jnp.float32)
    inputs_a = (base_a.astype(jnp.float32) * input_scale).astype(jnp.bfloat16)
    inputs_b = (base_b.astype(jnp.float32) * input_scale).astype(jnp.bfloat16)
    flat_a = inputs_a.reshape(all_rows, width)
    flat_b = inputs_b.reshape(all_rows, width)
    preact_a = jnp.dot(flat_a, layer_one, preferred_element_type=jnp.float32)
    offset = lax.axis_index("par") * quarter
    quarter_a = lax.dynamic_slice_in_dim(
        preact_a.reshape(windows, window_rows, hidden), offset, quarter, 1
    )
    quarter_inputs_b = lax.dynamic_slice_in_dim(inputs_b, offset, quarter, 1).reshape(
        windows * quarter, width
    )
    quarter_b = jnp.dot(quarter_inputs_b, layer_one, preferred_element_type=jnp.float32)
    quarter_pre = jnp.concatenate([quarter_a.reshape(windows * quarter, hidden), quarter_b], 0)
    quarter_out = network_tail(quarter_pre, layer_two, layer_three).reshape(
        2, windows, quarter, outputs
    )
    out_a_part = quarter_out[0]
    out_b_part = quarter_out[1]
    usable_part = lax.dynamic_slice_in_dim(usable, offset, quarter, 1)
    out_a, out_b = (
        lax.all_gather(out_a_part, "par", axis=1, tiled=True),
        lax.all_gather(out_b_part, "par", axis=1, tiled=True),
    )
    chosen_a = jnp.take(flat_a, swap_cols, axis=1).astype(jnp.float32)
    chosen_b = jnp.take(flat_b, swap_cols, axis=1).astype(jnp.float32)
    chosen_rows = jnp.take(layer_one, swap_cols, axis=0).astype(jnp.float32)
    preact_c = (
        preact_a[None, :, :]
        + jnp.transpose(chosen_b - chosen_a)[:, :, None] * chosen_rows[:, None, :]
    )
    out_c = network_tail(preact_c.reshape(groups * all_rows, hidden), layer_two, layer_three)
    differ = out_c.reshape(groups, windows, window_rows, outputs) - out_a[None]
    mask_rows = usable[:, :, None]
    mask_part = usable_part[:, :, None]
    pooled_sum = jnp.sum(mask_part * (out_a_part + out_b_part), axis=1)
    pooled_squares = jnp.sum(
        mask_part * (out_a_part * out_a_part + out_b_part * out_b_part), axis=1
    )
    total_part = (pooled_sum, pooled_squares)
    masked_d = differ * mask_rows[None]
    sum_b = jnp.sum(mask_rows * out_b, axis=1)[:, None, :]
    sum_d = jnp.transpose(jnp.sum(masked_d, axis=2), (1, 0, 2))
    squares_d = jnp.transpose(jnp.sum(masked_d * differ, axis=2), (1, 0, 2))
    cross_raw = jnp.transpose(jnp.sum(masked_d * out_b[None], axis=2), (1, 0, 2))
    group_part = (sum_b, sum_d, squares_d, cross_raw)

    def settle(total_piece, group_piece, ends_piece):
        total_sum, total_squares = lax.psum(total_piece, ("rows", "par"))
        group_b, group_d, group_squares, group_cross = lax.psum(group_piece, "rows")
        counts = ends_piece.astype(jnp.float32)[:, None, None]
        pooled_counts = 2.0 * counts[:, :, 0]
        total_mean = total_sum / pooled_counts
        total_state = (pooled_counts, total_mean, total_squares - total_sum * total_mean)
        mean_b = group_b / counts
        mean_d = group_d / counts
        group_state = (
            counts,
            mean_b,
            mean_d,
            group_squares - group_d * mean_d,
            group_cross - group_b * mean_d,
        )
        return (total_state, group_state)

    per_window = [
        settle(
            pick_window(total_part, window),
            pick_window(group_part, window),
            window_ends[window : window + 1],
        )
        for window in range(windows)
    ]
    settled = jax.tree.map(join_windows, *per_window)
    return conclude_states(settled[0], settled[1], windows)


def solution(mesh):
    in_specs = (P(None, "rows", None), P(None, "rows", None), P(), P(), P(), P(), P("par"), P())
    out_specs = (P(None, "par", None), P(None, "par", None), P())
    return jax.shard_map(local, mesh=mesh, in_specs=in_specs, out_specs=out_specs, check_vma=False)
```

profile of v0, /device:TPU:0, one launch (start us, length us, event | category | flops | bytes accessed | tf_op | source)
XLA Modules:
  0.0 131.8 jit_solution(2429451299486696578)
XLA Ops:
  7.2 0.0 copy-start
  7.2 0.0 all-reduce.4.cloned.1.call-start
  7.2 0.8 compare_and_fusion
  8.0 0.7 compare_select_fusion
  8.7 0.7 compare_convert_fusion
  9.4 0.1 copy.29
  9.5 0.8 fusion.14
  10.3 0.1 copy.26
  10.4 1.2 fusion.29
  11.6 1.2 fusion.31
  12.9 0.0 copy-done
  12.9 1.5 %fusion.11 = f32[16,128]{1,0:T(8,128)S(1)} fusion(bf16[1024,128]{1,0:T(8,128)(2,1)} %param.15, bf16[1024,1024]{1,0:T(8,128)(2,1)S(1)} %copy-done, f32[8,1024]{1,0:T(8,128)S(1)} %fusion.31, f32[8,1024]{1,0:T(8,128)S(1)} %reshape.400), kind=kOutput, calls=%fused_computation.28 | convolution fusion | flops 37928960 | bytes 2433024 | tf_op jit(solution)/shard_map/dot_general | solution.py:11
  14.4 6.2 %all_gather.7 = f32[4,8,128]{2,0,1:T(4,128)S(1)} all-gather(f32[4,2,128]{2,0,1:T(4,128)S(1)} %copy.30), channel_id=1, replica_groups=mesh['rows'=8,'par'=4] {'par'}, dimensions={1}, use_global_device_ids=true | all-gather | bytes 20480 | tf_op jit(solution)/shard_map/all_gather | solution.py:108
  20.7 0.1 multiply_reduce_fusion.1
  20.8 0.1 copy.25
  20.9 1.9 %gather_fusion = bf16[64,1024]{1,0:T(8,128)(2,1)S(1)} fusion(bf16[256,1024]{1,0:T(8,128)(2,1)} %param.13, s32[1024]{0:T(1024)S(1)} %pad_clamp_fusion), kind=kCustom, calls=%fused_computation.2 | custom fusion | bytes 262400 | tf_op jit(solution)/shard_map/jit(_take)/gather | solution.py:112
  22.8 0.6 gather_fusion.1
  23.4 0.6 gather_fusion.2
  24.1 0.1 subtract_bitcast_fusion
  24.2 0.1 mul.598
  24.2 0.6 slice_bitcast_fusion
  24.8 5.4 %all_gather.6 = f32[4,8,128]{2,0,1:T(4,128)S(1)} all-gather(f32[4,2,128]{2,0,1:T(4,128)S(1)} %copy.27), channel_id=1, replica_groups=mesh['rows'=8,'par'=4] {'par'}, dimensions={1}, use_global_device_ids=true | all-gather | bytes 20480 | tf_op jit(solution)/shard_map/all_gather | solution.py:107
  30.2 0.1 select_convert_fusion
  30.3 2.4 %fusion.6 = bf16[2048,1024]{1,0:T(8,128)(2,1)S(1)} fusion(f32[64,1024]{1,0:T(8,128)S(1)} %select_convert_fusion, f32[2048]{0:T(1024)S(1)} %mul.598, f32[32,1024]{1,0:T(8,128)S(1)} %fusion.29), kind=kLoop, calls=%fused_computation.10 | loop fusion | flops 14680064 | bytes 4595712 | tf_op jit(solution)/shard_map/convert_element_type | solution.py:8
  32.7 0.0 copy-start.1
  32.7 4.5 %fusion.30 = f32[2048,1024]{1,0:T(8,128)S(1)} fusion(bf16[2048,1024]{1,0:T(8,128)(2,1)S(1)} %fusion.6, bf16[1024,1024]{1,0:T(8,128)(2,1)S(1)} %copy-done), kind=kOutput, calls=%fused_computation.102 | convolution fusion | flops 4294967296 | bytes 14680064 | tf_op jit(solution)/shard_map/dot_general | solution.py:9
  37.3 0.0 copy-done.1
  37.3 0.0 copy-start.2
  37.3 3.0 %fusion.9 = (f32[64,4,128]{2,1,0:T(4,128)S(1)}, f32[64,4,128]{2,1,0:T(4,128)S(1)}, f32[64,4,128]{2,1,0:T(4,128)S(1)}) fusion(f32[4,8]{1,0:T(4,128)S(1)} %copy.29, f32[4,8,128]{2,1,0:T(8,128)S(1)} %copy.28, f32[4,8,128]{2,1,0:T(8,128)S(1)} %copy.31, bf16[1024,128]{1,0:T(8,128)(2,1)S(1)} %copy-done.1, f32[2048,1024]{1,0:T(8,128)S(1)} %fusion.30), kind=kOutput, calls=%fused_computation.17 | convolution fusion | flops 549093376 | bytes 9076864 | tf_op jit(solution)/shard_map/dot_general | solution.py:11
  40.4 0.7 fusion.22
  41.0 0.6 fusion.24
  41.7 0.7 fusion.23
  42.4 0.0 all-reduce.4.cloned.1.call-update
  42.4 0.0 copy-done.2
  42.4 0.6 fusion.28
  44.9 0.1 copy.34
  45.0 0.1 multiply_reduce_fusion.2
  45.1 40.8 %all-reduce = (f32[1,128]{1,0:T(1,128)S(1)}, f32[1,128]{1,0:T(1,128)S(1)}, f32[1,128]{1,0:T(1,128)S(1)}, f32[1,128]{1,0:T(1,128)S(1)}, f32[1,128]{1,0:T(1,128)S(...) all-reduce(f32[1,128]{1,0:T(1,128)S(1)} %get-tuple-element.105, ...), channel_id=1, replica_groups=mesh['rows'=8,'par'=4] {'rows','par'}, use_global_device_ids=true, to_apply=%region_13.15 | all-reduce | flops 1024 | bytes 8192 | tf_op jit(solution)/shard_map/psum | solution.py:134
  86.8 0.6 pad_maximum_fusion.3
  87.4 32.3 %all-reduce.4.cloned.1.call-done = (f32[1,64,128]{2,1,0:T(8,128)}, f32[1,1,128]{2,1,0:T(1,128)}, f32[1,1,128]{2,1,0:T(1,128)}, f32[1,64,128]{2,1,0:T(8,128)}, f3...) async-done(((f32[1,64,128]{2,1,0:T(8,128)}, ...) | async-done | bytes 395280 | tf_op jit(solution)/shard_map/psum | solution.py:135
  119.7 0.7 bitcast_add_fusion
  120.4 0.6 bitcast_subtract_fusion
  121.0 0.9 broadcast_divide_fusion.2
  121.9 0.8 multiply_divide_fusion.1
  122.8 0.8 multiply_divide_fusion
  123.6 0.7 pad_maximum_fusion.1
  124.3 0.7 pad_maximum_fusion
  (18 shorter events, 0.2 us)
Async XLA Ops:
  7.2 5.8 %copy-start = (bf16[1024,1024]{1,0:T(8,128)(2,1)S(1)}, bf16[1024,1024]{1,0:T(8,128)(2,1)}, u32[]{:S(2)}) copy-start(bf16[1024,1024]{1,0:T(8,128)(2,1)} %param.14) | copy-start | bytes 6291460
  7.2 112.5 %all-reduce.4.cloned.1.call-start = ((), (), s32[]{:S(2)}) async-start(), calls=%async_computation | async-start | bytes 790528 | tf_op jit(solution)/shard_map/psum | solution.py:135
  32.7 4.5 %copy-start.1 = (bf16[1024,128]{1,0:T(8,128)(2,1)S(1)}, bf16[1024,128]{1,0:T(8,128)(2,1)}, u32[]{:S(2)}) copy-start(bf16[1024,128]{1,0:T(8,128)(2,1)} %param.15) | copy-start | bytes 786436
  37.3 5.1 %copy-start.2 = (s32[4]{0:T(128)S(1)}, s32[4]{0:T(128)}, u32[]{:S(2)}) copy-start(s32[4]{0:T(128)} %param.17) | copy-start | bytes 52
Sparse Core Ops, SparseCore 0:
  42.5 77.1 all-reduce.3
where the time goes:
time: 133 us; the launch traced here: 132 us
  blocking collectives  52.4 us (39%)
  waiting for transfers between devices  32.3 us (24%)
  between operations  16.9 us (13%)
  other arithmetic  11.5 us (9%)
  matrix products  11.5 us (9%)
  local copies, waits for them, and re-layouts  7.03 us (5%)
    psum x1, blocking collectives, settle(): total_sum, total_squares = lax.psum(total_piece, ('rows', 'par'))  40.8 us
    psum x1, waiting for transfers between devices, settle(): group_b, group_d, group_squares, group_cross = lax.psum(group_piece, 'rows')  32.3 us
    all_gather x1, blocking collectives, local(): lax.all_gather(out_b_part, 'par', axis=1, tiled=True)  6.23 us
    all_gather x1, blocking collectives, local(): lax.all_gather(out_a_part, 'par', axis=1, tiled=True)  5.42 us
    dot_general x1, matrix products, network_tail(): jnp.dot(hidden_one, layer_two, preferred_element_type=jnp.float32)  4.53 us
    dot_general x2, matrix products, network_tail(): return jnp.dot(hidden_two, layer_three, preferred_element_type=jnp.float32)  4.52 us
  transfers between devices with their start and end apart: 1, of which 1 were waited for; matrix products, arithmetic and copies ran while one was open for 1% of the time, Pallas kernels for 0%

commit v1 on v0

v1 whole, which is shorter than its diff:
```python
import functools

import jax
import jax.numpy as jnp
from jax import lax
from jax.experimental import pallas as pl
from jax.experimental.pallas import tpu as pltpu
from jax.sharding import PartitionSpec as P

F32 = jnp.float32
BF16 = jnp.bfloat16
MESH = pl.DeviceIdType.MESH


def silu(value):
    half = 0.5 * value
    return half + half * jnp.tanh(half)


def dot(x, y):
    return jnp.dot(x, y, preferred_element_type=F32)


def dot_t(x, y):
    return lax.dot_general(x, y, (((1,), (1,)), ((), ())), preferred_element_type=F32)


def chunk_plan(n):
    unit = max(1, n // 8)
    sizes = [unit, unit, 2 * unit, 2 * unit, 2 * unit] if n >= 8 else [1] * n
    plan, start = [], 0
    for size in sizes:
        plan.append((start, size))
        start += size
    while start < n:
        plan.append((start, 1))
        start += 1
    return plan


def kernel(n, base_a, base_b, scale, cols, ends, w1_hbm, w2_hbm, w3_hbm,
           first, total, variance,
           w1, w2, w3, a_all, a_send, sel_all, sel_send, b_all, out_a_all, diff, onehot, h1, h2,
           w_sems, a_ss, a_rs, s_ss, s_rs, b_ss, b_rs, f_ss, f_rs, t_ss, t_rs):
    windows, window_rows, width = base_a.shape
    gq = first.shape[2]
    padded = onehot.shape[1]
    hidden = w2.shape[0]
    outputs = w3.shape[1]
    rows = windows * window_rows
    me = lax.axis_index("rows")

    loads = [pltpu.make_async_copy(src, dst, w_sems.at[i])
             for i, (src, dst) in enumerate(((w1_hbm, w1), (w2_hbm, w2), (w3_hbm, w3)))]
    for load in loads:
        load.start()

    barrier = pltpu.get_barrier_semaphore()
    for k in range(1, n):
        pl.semaphore_signal(barrier, inc=1, device_id={"rows": lax.rem(me + k, n)}, device_id_type=MESH)

    def send(src, dst, ss, rs, k):
        return pltpu.make_async_remote_copy(
            src_ref=src, dst_ref=dst, send_sem=ss.at[k], recv_sem=rs.at[k],
            device_id={"rows": lax.rem(me + n - k, n)}, device_id_type=MESH)

    factor = scale[...]
    own_a32 = (base_a[...].reshape(rows, width).astype(F32) * factor).astype(BF16).astype(F32)
    own_b = (base_b[...].reshape(rows, width).astype(F32) * factor).astype(BF16)
    a_send[...] = own_a32
    a_all[0] = own_a32
    lane = lax.broadcasted_iota(jnp.int32, (padded, width), 1)
    sub = lax.broadcasted_iota(jnp.int32, (padded, width), 0)
    for r in range(n):
        wanted = jnp.full((padded, width), cols[r * gq], jnp.int32)
        for g in range(1, gq):
            wanted = jnp.where(sub == g, cols[r * gq + g], wanted)
        onehot[r] = (lane == wanted).astype(F32)
    marks = onehot[...].reshape(n * padded, width).astype(BF16)
    chosen_b = dot_t(marks, own_b)
    sel_send[...] = chosen_b.reshape(n, padded, rows)
    sel_all[0] = sel_send[me]
    mark_own = onehot[me].astype(BF16)

    pl.semaphore_wait(barrier, n - 1)
    a_copies, s_copies = [], []
    for k in range(1, n):
        a_copies.append(send(a_send, a_all.at[k], a_ss, a_rs, k))
        a_copies[-1].start()
        s_copies.append(send(sel_send.at[lax.rem(me + n - k, n)], sel_all.at[k], s_ss, s_rs, k))
        s_copies[-1].start()

    loads[0].wait()
    swapped = dot(mark_own, w1[...])

    def tail(count):
        for c in range(0, hidden, 256):
            h2[:count, c : c + 256] = silu(dot(h1[:count, :], w2[:, c : c + 256])).astype(BF16)
        return dot(h2[:count, :], w3[...])

    b_copies = []
    for start, size in chunk_plan(n):
        if start > 0:
            for k in range(start, start + size):
                a_copies[k - 1].wait_recv()
                s_copies[k - 1].wait_recv()
        a_chunk = a_all[start : start + size].reshape(size * rows, width).astype(BF16)
        pre = dot(a_chunk, w1[...])
        chosen_a = dot_t(a_chunk, mark_own)
        base = 0
        for s in range(size):
            pre_s = pre[s * rows : (s + 1) * rows]
            delta = jnp.transpose(sel_all[start + s]) - chosen_a[s * rows : (s + 1) * rows]
            for g in range(gq):
                value = pre_s + delta[:, g : g + 1] * swapped[g : g + 1, :]
                h1[base : base + rows, :] = silu(value).astype(BF16)
                base += rows
            h1[base : base + rows, :] = silu(pre_s).astype(BF16)
            base += rows
        if start == 0:
            h1[base : base + rows, :] = silu(dot(own_b, w1[...])).astype(BF16)
            base += rows
            loads[1].wait()
            loads[2].wait()
        out = tail(base)
        base = 0
        for s in range(size):
            out_a = out[base + gq * rows : base + (gq + 1) * rows]
            out_a_all[start + s] = out_a
            for g in range(gq):
                diff[g, start + s] = out[base : base + rows] - out_a
                base += rows
            base += rows
        if start == 0:
            b_all[0] = out[base : base + rows]
            for k in range(1, n):
                b_copies.append(send(b_all.at[0], b_all.at[k], b_ss, b_rs, k))
                b_copies[-1].start()
    for copy in b_copies:
        copy.wait_recv()

    row_id = lax.broadcasted_iota(jnp.int32, (n, window_rows, outputs), 1)
    slot = lax.broadcasted_iota(jnp.int32, (n, window_rows, outputs), 0)
    position = lax.rem(me + slot, n) * window_rows + row_id
    former = None
    for w in range(windows):
        span = slice(w * window_rows, (w + 1) * window_rows)
        usable = (position < ends[w]).astype(F32)
        counts = jnp.full((1, outputs), ends[w], jnp.int32).astype(F32)
        inverse = 1.0 / counts
        oa = out_a_all[:, span, :]
        ob = b_all[:, span, :]

        def over_rows(x):
            return jnp.sum(jnp.sum(x, axis=0), axis=0, keepdims=True)

        pooled_mean = over_rows(usable * (oa + ob)) * (0.5 * inverse)
        dev_a = oa - pooled_mean
        dev_b = ob - pooled_mean
        pooled_spread = over_rows(usable * (dev_a * dev_a + dev_b * dev_b))
        mean_b = over_rows(usable * ob) * inverse
        centred_b = usable * (ob - mean_b)
        means, spreads, crosses = [], [], []
        for g in range(gq):
            d = diff[g, :, span, :]
            mean_d = over_rows(usable * d) * inverse
            centred = usable * (d - mean_d)
            means.append(mean_d)
            spreads.append(over_rows(centred * centred))
            crosses.append(over_rows(centred_b * centred))
        now = (counts, pooled_mean, pooled_spread, mean_b, jnp.concatenate(means, 0),
               jnp.concatenate(spreads, 0), jnp.concatenate(crosses, 0))
        if former is not None:
            n1, n2 = former[0], counts
            both = n1 + n2
            share = n2 / both
            weight = n1 * share
            e_p = now[1] - former[1]
            e_b = now[3] - former[3]
            e_d = now[4] - former[4]
            now = (both, former[1] + e_p * share, former[2] + now[2] + 2.0 * weight * e_p * e_p,
                   former[3] + e_b * share, former[4] + e_d * share,
                   former[5] + now[5] + e_d * e_d * weight, former[6] + now[6] + e_b * e_d * weight)
        former = now
        spread = now[2] / (2.0 * now[0])
        first[w, me] = now[6] / now[0] / spread
        total[w, me] = 0.5 * (now[5] / now[0] + now[4] * now[4]) / spread
        variance[w : w + 1, :] = spread

    f_copies = []
    for k in range(1, n):
        for ref, ss, rs in ((first, f_ss, f_rs), (total, t_ss, t_rs)):
            f_copies.append(send(ref.at[:, me], ref.at[:, me], ss, rs, k))
            f_copies[-1].start()
    for copy in f_copies:
        copy.wait_recv()
    for copy in a_copies + s_copies + b_copies + f_copies:
        copy.wait_send()


def solution(mesh):
    n = mesh.shape["rows"]

    def local(base_a, base_b, input_scale, layer_one, layer_two, layer_three, swap_cols, window_ends):
        windows, window_rows, width = base_a.shape
        groups = swap_cols.shape[0]
        gq = groups // n
        padded = -(-gq // 8) * 8
        hidden = layer_two.shape[0]
        outputs = layer_three.shape[1]
        rows = windows * window_rows
        most = max((size * (gq + 1) + (start == 0)) * rows for start, size in chunk_plan(n))
        vmem = pl.BlockSpec(memory_space=pltpu.VMEM)
        smem = pl.BlockSpec(memory_space=pltpu.SMEM)
        hbm = pl.BlockSpec(memory_space=pl.ANY)
        dma = pltpu.SemaphoreType.DMA
        first, total, variance = pl.pallas_call(
            functools.partial(kernel, n),
            out_shape=(
                jax.ShapeDtypeStruct((windows, n, gq, outputs), F32),
                jax.ShapeDtypeStruct((windows, n, gq, outputs), F32),
                jax.ShapeDtypeStruct((windows, outputs), F32),
            ),
            in_specs=[vmem, vmem, vmem, smem, smem, hbm, hbm, hbm],
            out_specs=(vmem, vmem, vmem),
            scratch_shapes=[
                pltpu.VMEM(layer_one.shape, BF16),
                pltpu.VMEM(layer_two.shape, BF16),
                pltpu.VMEM(layer_three.shape, BF16),
                pltpu.VMEM((n, rows, width), F32),
                pltpu.VMEM((rows, width), F32),
                pltpu.VMEM((n, padded, rows), F32),
                pltpu.VMEM((n, padded, rows), F32),
                pltpu.VMEM((n, rows, outputs), F32),
                pltpu.VMEM((n, rows, outputs), F32),
                pltpu.VMEM((gq, n, rows, outputs), F32),
                pltpu.VMEM((n, padded, width), F32),
                pltpu.VMEM((most, hidden), BF16),
                pltpu.VMEM((most, hidden), BF16),
                dma((3,)),
            ] + [dma((n,)) for _ in range(10)],
            compiler_params=pltpu.CompilerParams(
                collective_id=0, has_side_effects=True, vmem_limit_bytes=56 * 2**20
            ),
        )(base_a, base_b, input_scale.reshape(1, width), swap_cols, window_ends,
          layer_one, layer_two, layer_three)
        shape = (windows, groups, outputs)
        return first.reshape(shape), total.reshape(shape), variance

    in_specs = (P(None, "rows", None), P(None, "rows", None), P(), P(), P(), P(), P("par"), P())
    out_specs = (P(None, "par", None), P(None, "par", None), P())
    return jax.shard_map(local, mesh=mesh, in_specs=in_specs, out_specs=out_specs, check_vma=False)
```

time: 133 us -> 34.7 us (0.26)
  blocking collectives: 52.4 us -> 0 us
  waiting for transfers between devices: 32.3 us -> 0 us
  Pallas kernels: 0 us -> 29.4 us
  between operations: 16.9 us -> 0.64 us
  matrix products: 11.5 us -> 0 us
  other arithmetic: 11.5 us -> 0 us
  local copies, waits for them, and re-layouts: 7.03 us -> 4.38 us
    psum x1 -> x0, blocking collectives: 40.8 us -> none  [settle(): total_sum, total_squares = lax.psum(total_piece, ('rows', 'par'))]
    psum x1 -> x0, waiting for transfers between devices: 32.3 us -> none  [settle(): group_b, group_d, group_squares, group_cross = lax.psum(group_piece, 'rows')]
    pallas_call x0 -> x1, Pallas kernels: none -> 29.4 us  [local(): pl.pallas_call(functools.partial(kernel, n), out_shape=(jax.ShapeDtypeStr...]
    all_gather x2 -> x0, blocking collectives: 11.7 us -> none  [the longest x1 6.23 us: local(): lax.all_gather(out_b_part, 'par', axis=1, tiled=True)]
    dot_general x5 -> x0, matrix products: 11.5 us -> none  [the longest x1 4.53 us: network_tail(): jnp.dot(hidden_one, layer_two, preferred_element_type=jnp.float32)]
    unnamed x6 -> x3, local copies, waits for them, and re-layouts: 0.02 us -> 4.38 us
    slice x7 -> x0, local copies, waits for them, and re-layouts: 3.23 us -> none  [the longest x5 2.57 us: pick_window(): return tuple((member[window:window + 1] for member in states))]
    convert_element_type x3 -> x0, other arithmetic: 3.18 us -> none  [the longest x1 2.37 us: network_tail(): hidden_one = jax.nn.silu(first_pre).astype(jnp.bfloat16)]
  transfers between devices with their start and end apart: 1 -> 0, of which waited for: 1 -> 0; matrix products, arithmetic and copies ran while one was open for 1% -> 0% of each run, Pallas kernels for 0% -> 0%
where the time goes in v1:
time: 34.7 us; the launch traced here: 34.5 us
  Pallas kernels  29.4 us (85%)
  local copies, waits for them, and re-layouts  4.38 us (13%)
  between operations  0.64 us (2%)
    pallas_call x1, Pallas kernels, local(): pl.pallas_call(functools.partial(kernel, n), out_shape=(jax.ShapeDtypeStr...  29.4 us
    unnamed x3, local copies, waits for them, and re-layouts  4.38 us

profile of v1, /device:TPU:0, one launch (start us, length us, event | category | flops | bytes accessed | tf_op | source)
XLA Modules:
  0.0 34.5 jit_solution(5173249774457403205)
XLA Ops:
  0.6 29.4 %shard_map.103 = (f32[4,8,8,128]{3,2,1,0:T(8,128)}, f32[4,8,8,128]{3,2,1,0:T(8,128)}, f32[4,128]{1,0:T(4,128)}) custom-call(bf16[4,8,256]{2,1,0:T(8,128)(2,1)} %base_a.1, bf16[4,8,256]{2,1,0:T(8,128)(2,1)} %base_b.1, f32[1,256]{1,0:T(1,128)} %bitcast.5, s32[64]{0:T(128)} %cols.1, s32[4]{0:T(128)} %ends.1, bf16[256,1024]{1,0:T(8,128)(2,1)} %w1_hbm.1, ...), custom_call_target="tpu_custom_call" | custom-call | tf_op jit(solution)/shard_map/pallas_call | solution.py:217
  30.1 1.6 %copy.14 = f32[4,64,128]{2,1,0:T(8,128)} copy(f32[4,64,128]{2,1,0:T(8,128)} %bitcast.4) | data formatting | bytes 262144
  31.6 1.6 %copy.15 = f32[4,64,128]{2,1,0:T(8,128)} copy(f32[4,64,128]{2,1,0:T(8,128)} %bitcast.3) | data formatting | bytes 262144
  33.2 1.2 %copy.16 = f32[4,128]{1,0:T(4,128)} copy(f32[4,128]{1,0:T(4,128)} %get-tuple-element.14) | data formatting | bytes 4096
